TPU v7x, 256 devices: a whole 4x4x8 slice. The times are simulated.
256 devices in a mesh: copy: 2 (over core), fsdp: 32 (over z, y), tp: 4 (over x).
Axes of the slice: x: 4, y: 4, z: 8, core: 2. Of those that a mesh axis runs over, the one named last changes fastest.
Arguments:
- gradients: float32 [256, 128, 4096], P('copy', 'fsdp', 'tp'), parts along dimension 0, may hold values from -6 to 6
- momentum: float32 [256, 128, 4096], P('copy', 'fsdp', 'tp'), parts along dimension 0, may hold values from -6 to 6
- weights: float32 [256, 128, 4096], P('copy', 'fsdp', 'tp'), parts along dimension 0, may hold values from -0.1875 to 0.1875
Outputs:
- new_weights: float32 [256, 128, 4096], P('copy', 'fsdp', 'tp'), parts along dimension 0
- new_momentum: float32 [256, 128, 4096], P('copy', 'fsdp', 'tp'), parts along dimension 0
There are 2 independent parts, one for each index of `copy`. A program takes and returns all parts, laid end to end along the dimension named above; each array names one. Nothing has to cross between parts.
All inputs are finite; a program needn't handle non-finite values.
Results may differ from a plain program's by a relative error of at most 0.00014.
Values sent between devices are 32-bit elements; how exact they have to be, the bound alone decides.
A program may use at most 64 MiB of HBM per device.

v0:
```python
import functools

import jax
import jax.numpy as jnp
from jax import lax
from jax.experimental import pallas as pl
from jax.experimental.pallas import tpu as pltpu
from jax.sharding import PartitionSpec as P

ITERS = 4


hold_rate = 0.95
learn_rate = 0.9
decay_rate = 0.1

MESH = pl.DeviceIdType.MESH


def dot(a, b, contract=((1,), (0,))):
    return lax.dot_general(
        a,
        b,
        (contract, ((), ())),
        precision=lax.Precision.HIGHEST,
        preferred_element_type=jnp.float32,
    )


def mixing(gram):
    side = gram.shape[0]
    eye = (
        lax.broadcasted_iota(jnp.int32, (side, side), 0)
        == lax.broadcasted_iota(jnp.int32, (side, side), 1)
    ).astype(jnp.float32)
    scale = lax.rsqrt(jnp.sum(gram * eye, keepdims=True) + 1e-06)
    gram = gram * scale * scale
    total = scale * eye
    for step in range(ITERS):
        poly = 3.4445 * eye - 4.775 * gram + 2.0315 * dot(gram, gram)
        total = poly * scale if step == 0 else dot(poly, total)
        if step < ITERS - 1:
            gram = dot(poly, dot(gram, poly))
    return total


def plain(gradients, momentum, weights):
    new_momentum = hold_rate * momentum + gradients
    direction = hold_rate * new_momentum + gradients
    moved = lax.all_to_all(direction, "fsdp", split_axis=0, concat_axis=1, tiled=True)
    gram = jnp.einsum("mik,mjk->mij", moved, moved, precision=lax.Precision.HIGHEST)
    gram = lax.psum(gram, "tp")
    mixed = jax.vmap(mixing)(gram)
    iterate = jnp.einsum("mij,mjk->mik", mixed, moved, precision=lax.Precision.HIGHEST)
    back = lax.all_to_all(iterate, "fsdp", split_axis=1, concat_axis=0, tiled=True)
    new_weights = (1.0 - learn_rate * decay_rate) * weights - learn_rate * back
    return (new_weights, new_momentum)


def kernel(
    rows_of,
    cols_of,
    grad_hbm,
    mom_hbm,
    weight_hbm,
    new_weight_hbm,
    new_mom_hbm,
    grad,
    mom,
    weight,
    new_mom,
    direction,
    whole,
    grams,
    mixed,
    back,
    new_weight,
    load_sem,
    store_sem,
    store_weight_sem,
    there_send,
    there_recv,
    gram_send,
    gram_recv,
    back_send,
    back_recv,
):
    n, t = rows_of, cols_of
    me, mine = lax.axis_index("fsdp"), lax.axis_index("tp")
    mats, rows = grad.shape[1], grad.shape[2]
    half = n // 2
    flip = me // half
    spot = me + flip * (n - 1 - 2 * me)

    def peer(step):
        seen = lax.rem(spot + step, half) if step < half else n - 1 - (step - half)
        return seen + flip * (n - 1 - 2 * seen)

    def tp_peer(step):
        return lax.rem(mine + step, t)

    def block(owner):
        return pl.ds(pl.multiple_of(owner * rows, rows), rows)

    def load(k, which):
        pairs = ((grad_hbm, grad), (mom_hbm, mom), (weight_hbm, weight))
        source, target = pairs[which]
        return pltpu.make_async_copy(source.at[:, k], target.at[:, k], load_sem.at[which, k])

    def store_mom(k):
        return pltpu.make_async_copy(new_mom.at[:, k], new_mom_hbm.at[:, k], store_sem.at[k])

    def store_weight(k, owner):
        return pltpu.make_async_copy(
            new_weight.at[owner, k], new_weight_hbm.at[owner, k], store_weight_sem.at[owner, k]
        )

    def there(k, step):
        return pltpu.make_async_remote_copy(
            src_ref=direction.at[peer(step), k],
            dst_ref=whole.at[k, block(me)],
            send_sem=there_send.at[k, step],
            recv_sem=there_recv.at[k, me],
            device_id={"fsdp": peer(step)},
            device_id_type=MESH,
        )

    def there_landed(k, step):
        return pltpu.make_async_remote_copy(
            src_ref=direction.at[peer(step), k],
            dst_ref=whole.at[k, block(peer(step))],
            send_sem=there_send.at[k, step],
            recv_sem=there_recv.at[k, peer(step)],
            device_id={"fsdp": peer(step)},
            device_id_type=MESH,
        )

    def share(k, step):
        return pltpu.make_async_remote_copy(
            src_ref=grams.at[k, mine],
            dst_ref=grams.at[k, mine],
            send_sem=gram_send.at[k, step],
            recv_sem=gram_recv.at[k, mine],
            device_id={"tp": tp_peer(step)},
            device_id_type=MESH,
        )

    def share_landed(k, step):
        return pltpu.make_async_remote_copy(
            src_ref=grams.at[k, mine],
            dst_ref=grams.at[k, tp_peer(step)],
            send_sem=gram_send.at[k, step],
            recv_sem=gram_recv.at[k, tp_peer(step)],
            device_id={"tp": tp_peer(step)},
            device_id_type=MESH,
        )

    def home(k, step):
        return pltpu.make_async_remote_copy(
            src_ref=mixed.at[k, block(peer(step))],
            dst_ref=back.at[me, k],
            send_sem=back_send.at[k, step],
            recv_sem=back_recv.at[k, me],
            device_id={"fsdp": peer(step)},
            device_id_type=MESH,
        )

    def home_landed(k, step):
        return pltpu.make_async_remote_copy(
            src_ref=mixed.at[k, block(peer(step))],
            dst_ref=back.at[peer(step), k],
            send_sem=back_send.at[k, step],
            recv_sem=back_recv.at[k, peer(step)],
            device_id={"fsdp": peer(step)},
            device_id_type=MESH,
        )

    barrier = pltpu.get_barrier_semaphore()
    for step in range(1, n):
        pl.semaphore_signal(barrier, inc=1, device_id={"fsdp": peer(step)}, device_id_type=MESH)
    for step in range(1, t):
        pl.semaphore_signal(barrier, inc=1, device_id={"tp": tp_peer(step)}, device_id_type=MESH)
    for k in range(mats):
        load(k, 0).start()
        load(k, 1).start()

    def begin(k):
        load(k, 0).wait()
        load(k, 1).wait()
        fresh = hold_rate * mom[:, k] + grad[:, k]
        new_mom[:, k] = fresh
        direction[:, k] = hold_rate * fresh + grad[:, k]
        store_mom(k).start()

    begin(0)
    pl.semaphore_wait(barrier, n + t - 2)

    def send(k, carry):
        for step in range(1, n):
            there(k, step).start()
        whole[k, block(me)] = direction[me, k]

        @pl.when(k + 1 < mats)
        def _():
            begin(k + 1)

        return carry

    lax.fori_loop(0, mats, send, 0)
    for k in range(mats):
        load(k, 2).start()

    def work(k, carry):
        for step in range(1, n):
            there_landed(k, step).wait_recv()
        grams[k, mine] = dot(whole[k], whole[k], ((1,), (1,)))
        for step in range(1, t):
            share(k, step).start()
        for step in range(1, t):
            share_landed(k, step).wait_recv()
        gram = grams[k, 0]
        for other in range(1, t):
            gram = gram + grams[k, other]
        mixed[k] = dot(mixing(gram), whole[k])
        for step in range(1, n):
            home(k, step).start()
        back[me, k] = mixed[k, block(me)]
        return carry

    lax.fori_loop(0, mats, work, 0)

    def update(k, owner):
        new_weight[owner, k] = (1.0 - learn_rate * decay_rate) * weight[
            owner, k
        ] - learn_rate * back[owner, k]
        store_weight(k, owner).start()

    def finish(k, carry):
        load(k, 2).wait()
        update(k, me)
        for step in range(1, n):
            home_landed(k, step).wait_recv()
            update(k, peer(step))
        return carry

    lax.fori_loop(0, mats, finish, 0)

    def drain(k, carry):
        for step in range(1, n):
            there(k, step).wait_send()
            home(k, step).wait_send()
        for step in range(1, t):
            share(k, step).wait_send()
        for owner in range(n):
            store_weight(k, owner).wait()
        store_mom(k).wait()
        return carry

    lax.fori_loop(0, mats, drain, 0)


def write_kernel(new_weight, new_mom, new_weight_hbm, new_mom_hbm, sem):
    copies = [
        pltpu.make_async_copy(source.at[i], target.at[i], sem.at[which, i])
        for which, (source, target) in enumerate(
            ((new_mom, new_mom_hbm), (new_weight, new_weight_hbm))
        )
        for i in range(source.shape[0])
    ]
    for copy in copies:
        copy.start()
    for copy in copies:
        copy.wait()


def shards(n, t, gradients, momentum, weights):
    total, rows, cols = gradients.shape
    if rows % 8 or cols % 128 or n % 2 or t < 2:
        return plain(gradients, momentum, weights)
    mats, side = total // n, rows * n
    cut = (n, mats, rows, cols)
    held = pltpu.VMEM(cut, jnp.float32)
    full = pltpu.VMEM((mats, side, cols), jnp.float32)
    sems = lambda *shape: pltpu.SemaphoreType.DMA(shape)
    new_weights, new_momentum = pl.pallas_call(
        functools.partial(kernel, n, t),
        out_shape=[jax.ShapeDtypeStruct(cut, jnp.float32)] * 2,
        in_specs=[pl.BlockSpec(memory_space=pl.ANY)] * 3,
        out_specs=[pl.BlockSpec(memory_space=pl.ANY)] * 2,
        scratch_shapes=[
            held,
            held,
            held,
            held,
            held,
            full,
            pltpu.VMEM((mats, t, side, side), jnp.float32),
            full,
            held,
            held,
            sems(3, mats),
            sems(mats),
            sems(n, mats),
            sems(mats, n),
            sems(mats, n),
            sems(mats, t),
            sems(mats, t),
            sems(mats, n),
            sems(mats, n),
        ],
        compiler_params=pltpu.CompilerParams(
            collective_id=0, has_side_effects=True, vmem_limit_bytes=48 * 1024 * 1024
        ),
    )(gradients.reshape(cut), momentum.reshape(cut), weights.reshape(cut))
    new_weights, new_momentum = pl.pallas_call(
        write_kernel,
        out_shape=[jax.ShapeDtypeStruct(cut, jnp.float32)] * 2,
        in_specs=[pl.BlockSpec(memory_space=pl.ANY)] * 2,
        out_specs=[pl.BlockSpec(memory_space=pltpu.HBM)] * 2,
        scratch_shapes=[sems(2, n)],
        compiler_params=pltpu.CompilerParams(vmem_limit_bytes=1024 * 1024),
    )(new_weights, new_momentum)
    return (new_weights.reshape(total, rows, cols), new_momentum.reshape(total, rows, cols))


def solution(mesh):
    return jax.shard_map(
        functools.partial(shards, mesh.shape["fsdp"], mesh.shape["tp"]),
        mesh=mesh,
        in_specs=(P("copy", "fsdp", "tp"), P("copy", "fsdp", "tp"), P("copy", "fsdp", "tp")),
        out_specs=(P("copy", "fsdp", "tp"), P("copy", "fsdp", "tp")),
        check_vma=False,
    )
```

profile of v0, /device:TPU:1, one launch (start us, length us, event | category | flops | bytes accessed | tf_op | source)
XLA Modules:
  0.0 202.8 jit_solution(1208158559810278515)
XLA Ops:
  7.2 0.0 all-reduce.2.cloned.1.call-start
  7.2 4.6 %multiply_add_fusion = (f32[128,4,1024]{2,1,0:T(4,128)S(1)}, f32[128,4,1024]{2,1,0:T(4,128)}) fusion(f32[128,4,1024]{2,1,0:T(4,128)} %param.3, f32[128,4,1024]{2,1,0:T(4,128)} %param.4), kind=kLoop, calls=%fused_computation.2 | loop fusion | flops 2097152 | bytes 8388608 | tf_op jit(solution)/shard_map/add | solution.py:49
  11.8 60.5 %all_to_all.27 = f32[128,4,1024]{2,1,0:T(4,128)S(1)} all-to-all(f32[128,4,1024]{2,1,0:T(4,128)S(1)} %get-tuple-element.2), channel_id=1, replica_groups=mesh['copy'=2,'fsdp'=32,'tp'=4] {'fsdp'}, dimensions={0} | all-to-all | bytes 4194304 | tf_op jit(solution)/shard_map/all_to_all | solution.py:50
  72.3 1.5 copy.11
  73.9 2.0 all_to_all.23
  75.8 2.8 %fusion.12 = f32[4,128,128]{2,1,0:T(8,128)} fusion(f32[4,128,1024]{2,1,0:T(8,128)S(1)} %all_to_all.23), kind=kOutput, calls=%fused_computation.25 | convolution fusion | flops 805306368 | bytes 2359296 | tf_op jit(solution)/shard_map/mik,mjk->mij/dot_general | solution.py:51
  78.6 0.0 all-reduce.2.cloned.1.call-update
  78.7 44.1 %all-reduce.2.cloned.1.call-done = f32[4,128,128]{2,1,0:T(8,128)} async-done(((f32[4,128,128]{2,1,0:T(8,128)}), f32[4,128,128]{2,1,0:T(8,128)}) %all-reduce.2.cloned.1.call-update) | async-done | bytes 262160 | tf_op jit(solution)/shard_map/psum | solution.py:52
  122.8 1.1 multiply_reduce_fusion
  123.8 1.6 fusion.3
  125.5 1.4 fusion.6
  126.9 0.4 fusion.13
  127.3 0.4 fusion.2
  127.7 0.4 fusion.4
  128.1 0.4 fusion.14
  128.5 0.4 fusion.15
  128.9 0.4 fusion.1
  129.3 0.4 fusion.16
  129.7 0.4 fusion.18
  130.1 0.4 fusion.17
  130.5 0.4 fusion
  130.9 0.4 fusion.19
  131.3 1.9 fusion.20
  133.2 1.4 copy.8
  134.6 56.5 %all_to_all.28 = f32[4,128,1024]{2,0,1:T(4,128)S(1)} all-to-all(f32[4,128,1024]{2,0,1:T(4,128)S(1)} %copy.8), channel_id=1, replica_groups=mesh['copy'=2,'fsdp'=32,'tp'=4] {'fsdp'}, dimensions={1} | all-to-all | bytes 4194304 | tf_op jit(solution)/shard_map/all_to_all | solution.py:55
  191.1 0.6 broadcast_multiply_fusion
  191.7 0.0 copy-start
  191.7 1.8 copy.9
  193.5 0.0 copy-done
  193.5 2.5 %bitcast_subtract_fusion = f32[128,4,1024]{2,1,0:T(4,128)} fusion(f32[32,4,4,1024]{3,2,1,0:T(4,128)S(1)} %copy.9, f32[128,4,1024]{2,1,0:T(4,128)S(1)} %copy-done), kind=kLoop, calls=%fused_computation | loop fusion | flops 1048576 | bytes 6291456 | tf_op jit(solution)/shard_map/sub | solution.py:56
  (3 shorter events, 0.0 us)
Async XLA Ops:
  7.2 115.6 %all-reduce.2.cloned.1.call-start = ((), (), s32[]{:S(2)}) async-start(), calls=%async_computation.2 | async-start | bytes 524288 | tf_op jit(solution)/shard_map/psum | solution.py:52
  191.7 1.8 copy-start
Sparse Core Ops, SparseCore 0:
  78.7 43.9 all-reduce.1
where the time goes:
time: 206 us; the launch traced here: 203 us
  blocking collectives  117 us (57%)
  waiting for transfers between devices  44.1 us (21%)
  between operations  14.2 us (7%)
  matrix products  12 us (6%)
  other arithmetic  8.8 us (4%)
  local copies, waits for them, and re-layouts  6.68 us (3%)
    all_to_all x1, blocking collectives, plain(): lax.all_to_all(direction, 'fsdp', split_axis=0, concat_axis=1, tiled=True)  60.5 us
    all_to_all x1, blocking collectives, plain(): lax.all_to_all(iterate, 'fsdp', split_axis=1, concat_axis=0, tiled=True)  56.5 us
    psum x1, waiting for transfers between devices, plain(): gram = lax.psum(gram, 'tp')  44.1 us
    dot_general x13, matrix products, dot(): lax.dot_general(a, b, (contract, ((), ())), precision=lax.Precision.HIGHE...  7.33 us
    add x1, other arithmetic, plain(): direction = hold_rate * new_momentum + gradients  4.62 us
  transfers between devices with their start and end apart: 1, of which 1 were waited for; matrix products, arithmetic and copies ran while one was open for 0% of the time, Pallas kernels for 0%

commit v1 on v0

v1 whole, which is shorter than its diff:
```python
import functools

import jax
import jax.numpy as jnp
from jax import lax
from jax.experimental import pallas as pl
from jax.experimental.pallas import tpu as pltpu
from jax.sharding import PartitionSpec as P

ITERS = 4

hold_rate = 0.95
learn_rate = 0.9
decay_rate = 0.1

MESH = pl.DeviceIdType.MESH

Z, Y = 8, 4


def ring(step, size):
    return min(step, size - step)


OFFSETS = sorted(
    ((dz, dy) for dz in range(Z) for dy in range(Y) if dz or dy),
    key=lambda o: (-(ring(o[0], Z) + ring(o[1], Y)), o),
)


def dot(a, b, contract=((1,), (0,))):
    return lax.dot_general(
        a,
        b,
        (contract, ((), ())),
        precision=lax.Precision.HIGHEST,
        preferred_element_type=jnp.float32,
    )


def mixing(gram):
    side = gram.shape[0]
    eye = (
        lax.broadcasted_iota(jnp.int32, (side, side), 0)
        == lax.broadcasted_iota(jnp.int32, (side, side), 1)
    ).astype(jnp.float32)
    scale = lax.rsqrt(jnp.sum(gram * eye, keepdims=True) + 1e-06)
    gram = gram * scale * scale
    total = scale * eye
    for step in range(ITERS):
        poly = 3.4445 * eye - 4.775 * gram + 2.0315 * dot(gram, gram)
        total = poly * scale if step == 0 else dot(poly, total)
        if step < ITERS - 1:
            gram = dot(poly, dot(gram, poly))
    return total


def kernel(
    n,
    t,
    grad_hbm,
    mom_hbm,
    weight_hbm,
    new_weight,
    new_mom,
    grad,
    mom,
    weight,
    direction,
    whole,
    grams,
    mixed,
    back,
    load_sem,
    there_send,
    there_recv,
    gram_send,
    gram_recv,
    back_send,
    back_recv,
):
    me, mine = lax.axis_index("fsdp"), lax.axis_index("tp")
    z, y = me // Y, lax.rem(me, Y)
    mats, rows, cols = grad.shape[1:]
    side = n * rows
    steps = range(len(OFFSETS))

    def peer(step, sign=1):
        dz, dy = OFFSETS[step]
        if sign < 0:
            dz, dy = (Z - dz) % Z, (Y - dy) % Y
        return lax.rem(z + dz, Z) * Y + lax.rem(y + dy, Y)

    def tp_peer(step):
        return lax.rem(mine + step, t)

    def load(k, which):
        pairs = ((grad_hbm, grad), (mom_hbm, mom), (weight_hbm, weight))
        source, target = pairs[which]
        return pltpu.make_async_copy(source.at[:, k], target.at[:, k], load_sem.at[which, k])

    def there(k, step):
        return pltpu.make_async_remote_copy(
            src_ref=direction.at[peer(step), k],
            dst_ref=whole.at[k, me],
            send_sem=there_send.at[k, step],
            recv_sem=there_recv.at[k, step],
            device_id={"fsdp": peer(step)},
            device_id_type=MESH,
        )

    def there_landed(k, step):
        return pltpu.make_async_remote_copy(
            src_ref=direction.at[peer(step), k],
            dst_ref=whole.at[k, peer(step, -1)],
            send_sem=there_send.at[k, step],
            recv_sem=there_recv.at[k, step],
            device_id={"fsdp": peer(step)},
            device_id_type=MESH,
        )

    def share(k, step):
        return pltpu.make_async_remote_copy(
            src_ref=grams.at[k, mine],
            dst_ref=grams.at[k, mine],
            send_sem=gram_send.at[k, step],
            recv_sem=gram_recv.at[k, step],
            device_id={"tp": tp_peer(step)},
            device_id_type=MESH,
        )

    def share_landed(k, step):
        return pltpu.make_async_remote_copy(
            src_ref=grams.at[k, mine],
            dst_ref=grams.at[k, tp_peer(t - step)],
            send_sem=gram_send.at[k, step],
            recv_sem=gram_recv.at[k, step],
            device_id={"tp": tp_peer(step)},
            device_id_type=MESH,
        )

    def home(k, step):
        return pltpu.make_async_remote_copy(
            src_ref=mixed.at[k, peer(step)],
            dst_ref=back.at[me, k],
            send_sem=back_send.at[k, step],
            recv_sem=back_recv.at[k, step],
            device_id={"fsdp": peer(step)},
            device_id_type=MESH,
        )

    def home_landed(k, step):
        return pltpu.make_async_remote_copy(
            src_ref=mixed.at[k, peer(step)],
            dst_ref=back.at[peer(step, -1), k],
            send_sem=back_send.at[k, step],
            recv_sem=back_recv.at[k, step],
            device_id={"fsdp": peer(step)},
            device_id_type=MESH,
        )

    barrier = pltpu.get_barrier_semaphore()
    for step in steps:
        pl.semaphore_signal(barrier, inc=1, device_id={"fsdp": peer(step)}, device_id_type=MESH)
    for step in range(1, t):
        pl.semaphore_signal(barrier, inc=1, device_id={"tp": tp_peer(step)}, device_id_type=MESH)
    for k in range(mats):
        load(k, 0).start()
        load(k, 1).start()
    for k in range(mats):
        load(k, 2).start()

    def begin(k):
        load(k, 0).wait()
        load(k, 1).wait()
        fresh = hold_rate * mom[:, k] + grad[:, k]
        new_mom[:, k] = fresh
        direction[:, k] = hold_rate * fresh + grad[:, k]

    for k in range(mats):
        begin(k)
    pl.semaphore_wait(barrier, n + t - 2)

    def send(k, carry):
        for step in steps:
            there(k, step).start()
        whole[k, me] = direction[me, k]
        return carry

    lax.fori_loop(0, mats, send, 0)

    def work(k, carry):
        for step in steps:
            there_landed(k, step).wait_recv()
        matrix = whole[k].reshape(side, cols)
        grams[k, mine] = dot(matrix, matrix, ((1,), (1,)))
        for step in range(1, t):
            share(k, step).start()
        for step in range(1, t):
            share_landed(k, step).wait_recv()
        gram = grams[k, 0]
        for other in range(1, t):
            gram = gram + grams[k, other]
        result = dot(mixing(gram), whole[k].reshape(side, cols))
        mixed[k] = result.reshape(n, rows, cols)
        for step in steps:
            home(k, step).start()
        back[me, k] = mixed[k, me]
        return carry

    lax.fori_loop(0, mats, work, 0)

    def update(k, owner):
        new_weight[owner, k] = (1.0 - learn_rate * decay_rate) * weight[
            owner, k
        ] - learn_rate * back[owner, k]

    def finish(k, carry):
        load(k, 2).wait()
        update(k, me)
        for step in steps:
            home_landed(k, step).wait_recv()
            update(k, peer(step, -1))
        return carry

    lax.fori_loop(0, mats, finish, 0)

    def drain(k, carry):
        for step in steps:
            there(k, step).wait_send()
            home(k, step).wait_send()
        for step in range(1, t):
            share(k, step).wait_send()
        return carry

    lax.fori_loop(0, mats, drain, 0)


def write_kernel(new_weight, new_mom, new_weight_hbm, new_mom_hbm, sem):
    parts = 4
    copies = []
    for which, (source, target) in enumerate(
        ((new_mom, new_mom_hbm), (new_weight, new_weight_hbm))
    ):
        size = source.shape[0] // parts
        for i in range(parts):
            part = pl.ds(i * size, size)
            copies.append(
                pltpu.make_async_copy(source.at[part], target.at[part], sem.at[which, i])
            )
    for copy in copies:
        copy.start()
    for copy in copies:
        copy.wait()


def shards(n, t, gradients, momentum, weights):
    total, rows, cols = gradients.shape
    mats, side = total // n, rows * n
    cut = (n, mats, rows, cols)
    held = pltpu.VMEM(cut, jnp.float32)
    full = pltpu.VMEM((mats, n, rows, cols), jnp.float32)
    sems = lambda *shape: pltpu.SemaphoreType.DMA(shape)
    others = len(OFFSETS)
    new_weights, new_momentum = pl.pallas_call(
        functools.partial(kernel, n, t),
        out_shape=[jax.ShapeDtypeStruct(cut, jnp.float32)] * 2,
        in_specs=[pl.BlockSpec(memory_space=pl.ANY)] * 3,
        out_specs=[pl.BlockSpec(memory_space=pltpu.VMEM)] * 2,
        scratch_shapes=[
            held,
            held,
            held,
            held,
            full,
            pltpu.VMEM((mats, t, side, side), jnp.float32),
            full,
            held,
            sems(3, mats),
            sems(mats, others),
            sems(mats, others),
            sems(mats, t),
            sems(mats, t),
            sems(mats, others),
            sems(mats, others),
        ],
        compiler_params=pltpu.CompilerParams(
            collective_id=0, has_side_effects=True, vmem_limit_bytes=48 * 1024 * 1024
        ),
    )(gradients.reshape(cut), momentum.reshape(cut), weights.reshape(cut))
    new_weights, new_momentum = pl.pallas_call(
        write_kernel,
        out_shape=[jax.ShapeDtypeStruct(cut, jnp.float32)] * 2,
        in_specs=[pl.BlockSpec(memory_space=pl.ANY)] * 2,
        out_specs=[pl.BlockSpec(memory_space=pltpu.HBM)] * 2,
        scratch_shapes=[sems(2, 4)],
        compiler_params=pltpu.CompilerParams(vmem_limit_bytes=1024 * 1024),
    )(new_weights, new_momentum)
    return (new_weights.reshape(total, rows, cols), new_momentum.reshape(total, rows, cols))


def solution(mesh):
    return jax.shard_map(
        functools.partial(shards, mesh.shape["fsdp"], mesh.shape["tp"]),
        mesh=mesh,
        in_specs=(P("copy", "fsdp", "tp"), P("copy", "fsdp", "tp"), P("copy", "fsdp", "tp")),
        out_specs=(P("copy", "fsdp", "tp"), P("copy", "fsdp", "tp")),
        check_vma=False,
    )
```

time: 206 us -> 110 us (0.53); the launches traced: 203 us -> 110 us
  blocking collectives: 117 us -> 0 us
  Pallas kernels: 0 us -> 109 us
  waiting for transfers between devices: 44.1 us -> 0 us
  between operations: 14.2 us -> 0.64 us
  matrix products: 12 us -> 0 us
  other arithmetic: 8.8 us -> 0 us
  local copies, waits for them, and re-layouts: 6.68 us -> 0 us
    all_to_all x2 -> x0, blocking collectives: 117 us -> none  [the longest x1 60.5 us: plain(): lax.all_to_all(direction, 'fsdp', split_axis=0, concat_axis=1, tiled=True)]
    pallas_call x0 -> x2, Pallas kernels: none -> 109 us  [the longest x1 107 us: shards(): pl.pallas_call(functools.partial(kernel, n, t), out_shape=[jax.ShapeDtype...]
    psum x1 -> x0, waiting for transfers between devices: 44.1 us -> none  [plain(): gram = lax.psum(gram, 'tp')]
    dot_general x15 -> x0, matrix products: 12 us -> none  [the longest x13 7.33 us: dot(): lax.dot_general(a, b, (contract, ((), ())), precision=lax.Precision.HIGHE...]
    add x1 -> x0, other arithmetic: 4.62 us -> none  [plain(): direction = hold_rate * new_momentum + gradients]
    all_to_all x2 -> x0, local copies, waits for them, and re-layouts: 3.52 us -> none  [plain(): lax.all_to_all(direction, 'fsdp', split_axis=0, concat_axis=1, tiled=True)]
    sub x1 -> x0, other arithmetic: 2.48 us -> none  [plain(): new_weights = (1.0 - learn_rate * decay_rate) * weights - learn_rate * back]
  transfers between devices with their start and end apart: 1 -> 0, of which waited for: 1 -> 0; matrix products, arithmetic and copies ran while one was open for 0% -> 0% of each run, Pallas kernels for 0% -> 0%
where the time goes in v1:
time: 110 us
  Pallas kernels  109 us (99%)
    pallas_call x1, Pallas kernels, shards(): pl.pallas_call(functools.partial(kernel, n, t), out_shape=[jax.ShapeDtype...  107 us

profile of v1, /device:TPU:1, one launch (start us, length us, event | category | flops | bytes accessed | tf_op | source)
XLA Modules:
  0.0 109.7 jit_solution(11229461708480777041)
XLA Ops:
  0.6 107.0 %shard_map.50 = (f32[32,4,4,1024]{3,2,1,0:T(4,128)S(1)}, f32[32,4,4,1024]{3,2,1,0:T(4,128)S(1)}) custom-call(f32[32,4,4,1024]{3,2,1,0:T(4,128)} %bitcast.5, f32[32,4,4,1024]{3,2,1,0:T(4,128)} %bitcast.6, f32[32,4,4,1024]{3,2,1,0:T(4,128)} %bitcast.7), custom_call_target="tpu_custom_call" | custom-call | tf_op jit(solution)/shard_map/pallas_call | solution.py:265
  107.6 2.1 %shard_map.51 = (f32[32,4,4,1024]{3,2,1,0:T(4,128)}, f32[32,4,4,1024]{3,2,1,0:T(4,128)}) custom-call(f32[32,4,4,1024]{3,2,1,0:T(4,128)S(1)} %get-tuple-element.6.new_weight, f32[32,4,4,1024]{3,2,1,0:T(4,128)S(1)} %get-tuple-element.7.new_mom), custom_call_target="tpu_custom_call" | custom-call | tf_op jit(solution)/shard_map/pallas_call | solution.py:291

commit v2 on v1

--- a/solution.py
+++ b/solution.py
@@ -85,10 +85,8 @@
     side = n * rows
     steps = range(len(OFFSETS))
 
-    def peer(step, sign=1):
+    def peer(step):
         dz, dy = OFFSETS[step]
-        if sign < 0:
-            dz, dy = (Z - dz) % Z, (Y - dy) % Y
         return lax.rem(z + dz, Z) * Y + lax.rem(y + dy, Y)
 
     def tp_peer(step):
@@ -103,19 +101,20 @@
         return pltpu.make_async_remote_copy(
             src_ref=direction.at[peer(step), k],
             dst_ref=whole.at[k, me],
-            send_sem=there_send.at[k, step],
-            recv_sem=there_recv.at[k, step],
+            send_sem=there_send.at[k],
+            recv_sem=there_recv.at[k],
             device_id={"fsdp": peer(step)},
             device_id_type=MESH,
         )
 
-    def there_landed(k, step):
-        return pltpu.make_async_remote_copy(
-            src_ref=direction.at[peer(step), k],
-            dst_ref=whole.at[k, peer(step, -1)],
-            send_sem=there_send.at[k, step],
-            recv_sem=there_recv.at[k, step],
-            device_id={"fsdp": peer(step)},
+    def there_all(k):
+        some = pl.ds(0, n - 1)
+        return pltpu.make_async_remote_copy(
+            src_ref=direction.at[some, k],
+            dst_ref=whole.at[k, some],
+            send_sem=there_send.at[k],
+            recv_sem=there_recv.at[k],
+            device_id={"fsdp": peer(0)},
             device_id_type=MESH,
         )
 
@@ -123,19 +122,20 @@
         return pltpu.make_async_remote_copy(
             src_ref=grams.at[k, mine],
             dst_ref=grams.at[k, mine],
-            send_sem=gram_send.at[k, step],
-            recv_sem=gram_recv.at[k, step],
+            send_sem=gram_send.at[k],
+            recv_sem=gram_recv.at[k],
             device_id={"tp": tp_peer(step)},
             device_id_type=MESH,
         )
 
-    def share_landed(k, step):
-        return pltpu.make_async_remote_copy(
-            src_ref=grams.at[k, mine],
-            dst_ref=grams.at[k, tp_peer(t - step)],
-            send_sem=gram_send.at[k, step],
-            recv_sem=gram_recv.at[k, step],
-            device_id={"tp": tp_peer(step)},
+    def share_all(k):
+        some = pl.ds(0, t - 1)
+        return pltpu.make_async_remote_copy(
+            src_ref=grams.at[k, some],
+            dst_ref=grams.at[k, some],
+            send_sem=gram_send.at[k],
+            recv_sem=gram_recv.at[k],
+            device_id={"tp": tp_peer(1)},
             device_id_type=MESH,
         )
 
@@ -143,19 +143,20 @@
         return pltpu.make_async_remote_copy(
             src_ref=mixed.at[k, peer(step)],
             dst_ref=back.at[me, k],
-            send_sem=back_send.at[k, step],
-            recv_sem=back_recv.at[k, step],
+            send_sem=back_send.at[k],
+            recv_sem=back_recv.at[k],
             device_id={"fsdp": peer(step)},
             device_id_type=MESH,
         )
 
-    def home_landed(k, step):
-        return pltpu.make_async_remote_copy(
-            src_ref=mixed.at[k, peer(step)],
-            dst_ref=back.at[peer(step, -1), k],
-            send_sem=back_send.at[k, step],
-            recv_sem=back_recv.at[k, step],
-            device_id={"fsdp": peer(step)},
+    def home_all(k):
+        some = pl.ds(0, n - 1)
+        return pltpu.make_async_remote_copy(
+            src_ref=mixed.at[k, some],
+            dst_ref=back.at[some, k],
+            send_sem=back_send.at[k],
+            recv_sem=back_recv.at[k],
+            device_id={"fsdp": peer(0)},
             device_id_type=MESH,
         )
 
@@ -190,14 +191,12 @@
     lax.fori_loop(0, mats, send, 0)
 
     def work(k, carry):
-        for step in steps:
-            there_landed(k, step).wait_recv()
+        there_all(k).wait_recv()
         matrix = whole[k].reshape(side, cols)
         grams[k, mine] = dot(matrix, matrix, ((1,), (1,)))
         for step in range(1, t):
             share(k, step).start()
-        for step in range(1, t):
-            share_landed(k, step).wait_recv()
+        share_all(k).wait_recv()
         gram = grams[k, 0]
         for other in range(1, t):
             gram = gram + grams[k, other]
@@ -210,27 +209,18 @@
 
     lax.fori_loop(0, mats, work, 0)
 
-    def update(k, owner):
-        new_weight[owner, k] = (1.0 - learn_rate * decay_rate) * weight[
-            owner, k
-        ] - learn_rate * back[owner, k]
-
     def finish(k, carry):
         load(k, 2).wait()
-        update(k, me)
-        for step in steps:
-            home_landed(k, step).wait_recv()
-            update(k, peer(step, -1))
+        there_all(k).wait_send()
+        share_all(k).wait_send()
+        home_all(k).wait_recv()
+        new_weight[:, k] = (1.0 - learn_rate * decay_rate) * weight[:, k] - learn_rate * back[:, k]
         return carry
 
     lax.fori_loop(0, mats, finish, 0)
 
     def drain(k, carry):
-        for step in steps:
-            there(k, step).wait_send()
-            home(k, step).wait_send()
-        for step in range(1, t):
-            share(k, step).wait_send()
+        home_all(k).wait_send()
         return carry
 
     lax.fori_loop(0, mats, drain, 0)
@@ -261,7 +251,6 @@
     held = pltpu.VMEM(cut, jnp.float32)
     full = pltpu.VMEM((mats, n, rows, cols), jnp.float32)
     sems = lambda *shape: pltpu.SemaphoreType.DMA(shape)
-    others = len(OFFSETS)
     new_weights, new_momentum = pl.pallas_call(
         functools.partial(kernel, n, t),
         out_shape=[jax.ShapeDtypeStruct(cut, jnp.float32)] * 2,
@@ -277,12 +266,12 @@
             full,
             held,
             sems(3, mats),
-            sems(mats, others),
-            sems(mats, others),
-            sems(mats, t),
-            sems(mats, t),
-            sems(mats, others),
-            sems(mats, others),
+            sems(mats),
+            sems(mats),
+            sems(mats),
+            sems(mats),
+            sems(mats),
+            sems(mats),
         ],
         compiler_params=pltpu.CompilerParams(
             collective_id=0, has_side_effects=True, vmem_limit_bytes=48 * 1024 * 1024

time: 110 us -> 105 us (0.955)
  Pallas kernels: 109 us -> 104 us
    pallas_call x1, Pallas kernels: 107 us -> 102 us  [shards(): pl.pallas_call(functools.partial(kernel, n, t), out_shape=[jax.ShapeDtype...]
where the time goes in v2:
time: 105 us
  Pallas kernels  104 us (99%)
    pallas_call x1, Pallas kernels, shards(): pl.pallas_call(functools.partial(kernel, n, t), out_shape=[jax.ShapeDtype...  102 us

profile of v2, /device:TPU:1, one launch (start us, length us, event | category | flops | bytes accessed | tf_op | source)
XLA Modules:
  0.0 104.9 jit_solution(2811326166803213374)
XLA Ops:
  0.6 102.1 %shard_map.50 = (f32[32,4,4,1024]{3,2,1,0:T(4,128)S(1)}, f32[32,4,4,1024]{3,2,1,0:T(4,128)S(1)}) custom-call(f32[32,4,4,1024]{3,2,1,0:T(4,128)} %bitcast.5, f32[32,4,4,1024]{3,2,1,0:T(4,128)} %bitcast.6, f32[32,4,4,1024]{3,2,1,0:T(4,128)} %bitcast.7), custom_call_target="tpu_custom_call" | custom-call | tf_op jit(solution)/shard_map/pallas_call | solution.py:254
  102.8 2.1 %shard_map.51 = (f32[32,4,4,1024]{3,2,1,0:T(4,128)}, f32[32,4,4,1024]{3,2,1,0:T(4,128)}) custom-call(f32[32,4,4,1024]{3,2,1,0:T(4,128)S(1)} %get-tuple-element.6.new_weight, f32[32,4,4,1024]{3,2,1,0:T(4,128)S(1)} %get-tuple-element.7.new_mom), custom_call_target="tpu_custom_call" | custom-call | tf_op jit(solution)/shard_map/pallas_call | solution.py:280

commit v3 on v2

--- a/solution.py
+++ b/solution.py
@@ -78,6 +78,9 @@
     gram_recv,
     back_send,
     back_recv,
+    below,
+    above,
+    lines,
 ):
     me, mine = lax.axis_index("fsdp"), lax.axis_index("tp")
     z, y = me // Y, lax.rem(me, Y)
@@ -85,9 +88,11 @@
     side = n * rows
     steps = range(len(OFFSETS))
 
+    def member(dz, dy):
+        return lax.rem(z + dz % Z, Z) * Y + lax.rem(y + dy % Y, Y)
+
     def peer(step):
-        dz, dy = OFFSETS[step]
-        return lax.rem(z + dz, Z) * Y + lax.rem(y + dy, Y)
+        return member(*OFFSETS[step])
 
     def tp_peer(step):
         return lax.rem(mine + step, t)
@@ -97,13 +102,13 @@
         source, target = pairs[which]
         return pltpu.make_async_copy(source.at[:, k], target.at[:, k], load_sem.at[which, k])
 
-    def there(k, step):
-        return pltpu.make_async_remote_copy(
-            src_ref=direction.at[peer(step), k],
+    def there(k, dz, dy):
+        return pltpu.make_async_remote_copy(
+            src_ref=direction.at[member(dz, dy), k],
             dst_ref=whole.at[k, me],
             send_sem=there_send.at[k],
             recv_sem=there_recv.at[k],
-            device_id={"fsdp": peer(step)},
+            device_id={"fsdp": member(dz, dy)},
             device_id_type=MESH,
         )
 
@@ -160,9 +165,24 @@
             device_id_type=MESH,
         )
 
+    def tell(sem, dz, dy):
+        pl.semaphore_signal(sem, inc=1, device_id={"fsdp": member(dz, dy)}, device_id_type=MESH)
+
+    def begin(k):
+        load(k, 0).wait()
+        load(k, 1).wait()
+        fresh = hold_rate * mom[:, k] + grad[:, k]
+        new_mom[:, k] = fresh
+        direction[:, k] = hold_rate * fresh + grad[:, k]
+
+    def along_z(ks, *distances):
+        for distance in distances:
+            for k in ks:
+                there(k, distance, 0).start()
+
     barrier = pltpu.get_barrier_semaphore()
-    for step in steps:
-        pl.semaphore_signal(barrier, inc=1, device_id={"fsdp": peer(step)}, device_id_type=MESH)
+    for dz, dy in ((1, 0), (-1, 0), (0, 1), (0, -1), (0, 2)):
+        tell(barrier, dz, dy)
     for step in range(1, t):
         pl.semaphore_signal(barrier, inc=1, device_id={"tp": tp_peer(step)}, device_id_type=MESH)
     for k in range(mats):
@@ -170,25 +190,52 @@
         load(k, 1).start()
     for k in range(mats):
         load(k, 2).start()
-
-    def begin(k):
-        load(k, 0).wait()
-        load(k, 1).wait()
-        fresh = hold_rate * mom[:, k] + grad[:, k]
-        new_mom[:, k] = fresh
-        direction[:, k] = hold_rate * fresh + grad[:, k]
-
-    for k in range(mats):
-        begin(k)
-    pl.semaphore_wait(barrier, n + t - 2)
+    begin(0)
+    pl.semaphore_wait(barrier, 2 + (Y - 1) + (t - 1))
+    tell(below.at[0], 1, 0)
+    tell(above.at[0], -1, 0)
+    along_z((0,), 1, -1)
+    begin(1)
+    along_z((1,), 1, -1)
+    pl.semaphore_wait(below.at[0], 1)
+    tell(below.at[1], 1, 0)
+    pl.semaphore_wait(above.at[0], 1)
+    tell(above.at[1], -1, 0)
+    along_z((0, 1), -2, 2)
+    begin(2)
+    along_z((2,), 1, -1, -2, 2)
+    pl.semaphore_wait(below.at[1], 1)
+    tell(below.at[2], 1, 0)
+    pl.semaphore_wait(above.at[1], 1)
+    along_z((0, 1, 2), -3, 3)
+    begin(3)
+    along_z((3,), 1, -1, -2, 2, -3, 3)
+    pl.semaphore_wait(below.at[2], 1)
+    for dy in range(1, Y):
+        tell(lines.at[dy - 1], 0, dy)
+    along_z(range(mats), Z // 2)
+    for dy in range(1, Y):
+        for k in range(mats):
+            there(k, 0, dy).start()
+    for dy in (1, 3, 2):
+        pl.semaphore_wait(lines.at[dy - 1], 1)
+        for dz, other in OFFSETS:
+            if dz and other == Y - dy:
+                there(0, dz, other).start()
 
     def send(k, carry):
-        for step in steps:
-            there(k, step).start()
+        for dz, dy in OFFSETS:
+            if dz and dy:
+                there(k, dz, dy).start()
+        return carry
+
+    lax.fori_loop(1, mats, send, 0)
+
+    def own(k, carry):
         whole[k, me] = direction[me, k]
         return carry
 
-    lax.fori_loop(0, mats, send, 0)
+    lax.fori_loop(0, mats, own, 0)
 
     def work(k, carry):
         there_all(k).wait_recv()
@@ -272,6 +319,9 @@
             sems(mats),
             sems(mats),
             sems(mats),
+            pltpu.SemaphoreType.REGULAR((Z // 2 - 1,)),
+            pltpu.SemaphoreType.REGULAR((Z // 2 - 2,)),
+            pltpu.SemaphoreType.REGULAR((Y - 1,)),
         ],
         compiler_params=pltpu.CompilerParams(
             collective_id=0, has_side_effects=True, vmem_limit_bytes=48 * 1024 * 1024

time: 105 us -> 104 us (level)
  no operation moved by 1% of the time
where the time goes in v3:
time: 104 us
  Pallas kernels  103 us (99%)
    pallas_call x1, Pallas kernels, shards(): pl.pallas_call(functools.partial(kernel, n, t), out_shape=[jax.ShapeDtype...  101 us

profile of v3, /device:TPU:1, one launch (start us, length us, event | category | flops | bytes accessed | tf_op | source)
XLA Modules:
  0.0 103.8 jit_solution(5889864565467587758)
XLA Ops:
  0.6 101.1 %shard_map.50 = (f32[32,4,4,1024]{3,2,1,0:T(4,128)S(1)}, f32[32,4,4,1024]{3,2,1,0:T(4,128)S(1)}) custom-call(f32[32,4,4,1024]{3,2,1,0:T(4,128)} %bitcast.5, f32[32,4,4,1024]{3,2,1,0:T(4,128)} %bitcast.6, f32[32,4,4,1024]{3,2,1,0:T(4,128)} %bitcast.7), custom_call_target="tpu_custom_call" | custom-call | tf_op jit(solution)/shard_map/pallas_call | solution.py:301
  101.8 2.1 %shard_map.51 = (f32[32,4,4,1024]{3,2,1,0:T(4,128)}, f32[32,4,4,1024]{3,2,1,0:T(4,128)}) custom-call(f32[32,4,4,1024]{3,2,1,0:T(4,128)S(1)} %get-tuple-element.6.new_weight, f32[32,4,4,1024]{3,2,1,0:T(4,128)S(1)} %get-tuple-element.7.new_mom), custom_call_target="tpu_custom_call" | custom-call | tf_op jit(solution)/shard_map/pallas_call | solution.py:330

commit v4 on v3

--- a/solution.py
+++ b/solution.py
@@ -86,7 +86,9 @@
     z, y = me // Y, lax.rem(me, Y)
     mats, rows, cols = grad.shape[1:]
     side = n * rows
-    steps = range(len(OFFSETS))
+    hops = [ring(dz, Z) + ring(dy, Y) for dz, dy in OFFSETS]
+    far = [step for step, count in enumerate(hops) if count > 2]
+    close = [step for step, count in enumerate(hops) if count <= 2]
 
     def member(dz, dy):
         return lax.rem(z + dz % Z, Z) * Y + lax.rem(y + dy % Y, Y)
@@ -249,8 +251,20 @@
             gram = gram + grams[k, other]
         result = dot(mixing(gram), whole[k].reshape(side, cols))
         mixed[k] = result.reshape(n, rows, cols)
-        for step in steps:
+        for step in far:
             home(k, step).start()
+
+        @pl.when(k < mats - 2)
+        def _():
+            for step in close:
+                home(k, step).start()
+
+        @pl.when(k == mats - 1)
+        def _():
+            for step in close:
+                for each in (mats - 2, mats - 1):
+                    home(each, step).start()
+
         back[me, k] = mixed[k, me]
         return carry
 
@@ -274,17 +288,10 @@
 
 
 def write_kernel(new_weight, new_mom, new_weight_hbm, new_mom_hbm, sem):
-    parts = 4
-    copies = []
-    for which, (source, target) in enumerate(
-        ((new_mom, new_mom_hbm), (new_weight, new_weight_hbm))
-    ):
-        size = source.shape[0] // parts
-        for i in range(parts):
-            part = pl.ds(i * size, size)
-            copies.append(
-                pltpu.make_async_copy(source.at[part], target.at[part], sem.at[which, i])
-            )
+    copies = [
+        pltpu.make_async_copy(new_mom, new_mom_hbm, sem.at[0]),
+        pltpu.make_async_copy(new_weight, new_weight_hbm, sem.at[1]),
+    ]
     for copy in copies:
         copy.start()
     for copy in copies:
@@ -332,7 +339,7 @@
         out_shape=[jax.ShapeDtypeStruct(cut, jnp.float32)] * 2,
         in_specs=[pl.BlockSpec(memory_space=pl.ANY)] * 2,
         out_specs=[pl.BlockSpec(memory_space=pltpu.HBM)] * 2,
-        scratch_shapes=[sems(2, 4)],
+        scratch_shapes=[sems(2)],
         compiler_params=pltpu.CompilerParams(vmem_limit_bytes=1024 * 1024),
     )(new_weights, new_momentum)
     return (new_weights.reshape(total, rows, cols), new_momentum.reshape(total, rows, cols))

time: 104 us -> 103 us (level)
  no operation moved by 1% of the time
where the time goes in v4:
time: 103 us
  Pallas kernels  103 us (100%)
    pallas_call x1, Pallas kernels, shards(): pl.pallas_call(functools.partial(kernel, n, t), out_shape=[jax.ShapeDtype...  101 us

profile of v4, /device:TPU:1, one launch (start us, length us, event | category | flops | bytes accessed | tf_op | source)
XLA Modules:
  0.0 103.4 jit_solution(13938696243157871215)
XLA Ops:
  0.6 100.7 %shard_map.50 = (f32[32,4,4,1024]{3,2,1,0:T(4,128)S(1)}, f32[32,4,4,1024]{3,2,1,0:T(4,128)S(1)}) custom-call(f32[32,4,4,1024]{3,2,1,0:T(4,128)} %bitcast.5, f32[32,4,4,1024]{3,2,1,0:T(4,128)} %bitcast.6, f32[32,4,4,1024]{3,2,1,0:T(4,128)} %bitcast.7), custom_call_target="tpu_custom_call" | custom-call | tf_op jit(solution)/shard_map/pallas_call | solution.py:308
  101.4 2.0 %shard_map.51 = (f32[32,4,4,1024]{3,2,1,0:T(4,128)}, f32[32,4,4,1024]{3,2,1,0:T(4,128)}) custom-call(f32[32,4,4,1024]{3,2,1,0:T(4,128)S(1)} %get-tuple-element.6.new_weight, f32[32,4,4,1024]{3,2,1,0:T(4,128)S(1)} %get-tuple-element.7.new_mom), custom_call_target="tpu_custom_call" | custom-call | tf_op jit(solution)/shard_map/pallas_call | solution.py:337

commit v5 on v4

--- a/solution.py
+++ b/solution.py
@@ -261,9 +261,15 @@
 
         @pl.when(k == mats - 1)
         def _():
-            for step in close:
-                for each in (mats - 2, mats - 1):
-                    home(each, step).start()
+            def round_of(first):
+                for step in close:
+                    @pl.when((peer(step) < Y) == first)
+                    def _():
+                        for each in (mats - 2, mats - 1):
+                            home(each, step).start()
+
+            round_of(True)
+            round_of(False)
 
         back[me, k] = mixed[k, me]
         return carry

time: 103 us -> 103 us (level)
  no operation moved by 1% of the time
where the time goes in v5:
time: 103 us
  Pallas kernels  102 us (99%)
    pallas_call x1, Pallas kernels, shards(): pl.pallas_call(functools.partial(kernel, n, t), out_shape=[jax.ShapeDtype...  100 us

profile of v5, /device:TPU:1, one launch (start us, length us, event | category | flops | bytes accessed | tf_op | source)
XLA Modules:
  0.0 103.1 jit_solution(6816994911380802725)
XLA Ops:
  0.6 100.4 %shard_map.50 = (f32[32,4,4,1024]{3,2,1,0:T(4,128)S(1)}, f32[32,4,4,1024]{3,2,1,0:T(4,128)S(1)}) custom-call(f32[32,4,4,1024]{3,2,1,0:T(4,128)} %bitcast.5, f32[32,4,4,1024]{3,2,1,0:T(4,128)} %bitcast.6, f32[32,4,4,1024]{3,2,1,0:T(4,128)} %bitcast.7), custom_call_target="tpu_custom_call" | custom-call | tf_op jit(solution)/shard_map/pallas_call | solution.py:314
  101.0 2.0 %shard_map.51 = (f32[32,4,4,1024]{3,2,1,0:T(4,128)}, f32[32,4,4,1024]{3,2,1,0:T(4,128)}) custom-call(f32[32,4,4,1024]{3,2,1,0:T(4,128)S(1)} %get-tuple-element.6.new_weight, f32[32,4,4,1024]{3,2,1,0:T(4,128)S(1)} %get-tuple-element.7.new_mom), custom_call_target="tpu_custom_call" | custom-call | tf_op jit(solution)/shard_map/pallas_call | solution.py:343
